TPU v7x, 32 devices: a whole 2x2x4 slice. The times are simulated.
32 devices in a mesh: var: 8 (over z, core), samp: 4 (over y, x).
Axes of the slice: x: 2, y: 2, z: 4, core: 2. Of those that a mesh axis runs over, the one named last changes fastest.
Arguments:
- geno: bfloat16 [8192, 16384], P('samp', 'var'), may hold values from -5 to 5
- scale_index: int32 [64, 16384], P('samp', 'var'), may hold values from 0 to 15
- scale_table: float32 [16], replicated, may hold values from 0.25 to 4
- residual: float32 [8, 8192], P(None, 'samp'), may hold values from -6 to 6
- beta_active: float32 [8, 3584], P(None, 'var'), may hold values from -6 to 6
- block_inverse: float32 [16, 256, 256], P('var'), may hold values from -1 to 4
- active_ids: int32 [3584], P('var'), may hold values from 0 to 16383, as said below
- admit_ids: int32 [512], P('var'), may hold values from 0 to 16383, as said below
Outputs:
- scores: float32 [8, 16384], P(None, 'var')
- coefficients: float32 [8, 4096], P(None, 'var')
- residual_out: float32 [8, 8192], P(None, 'samp')
Inputs may be any that keep to these rules, and one draw needn't show every extreme that they name: Variant ids, all different from one another and from those of admit_ids. The fitting slots of one index of var are its 448 entries of active_ids followed by its 64 entries of admit_ids; of these 512 slots at most 128 name variants held by any one index of var, and for every index of var some one holder reaches exactly 128. `admit_ids`: variant ids, as for active_ids.
All inputs are finite; a program needn't handle non-finite values.
Results may differ from a plain program's by a relative error of at most 0.004.
Values may be sent and summed in bfloat16 or wider, within the bound.
A program may use at most 128 MiB of HBM per device.

v0:
```python
import math

import jax
import jax.numpy as jnp
from jax import lax
from jax.sharding import PartitionSpec as P

PASSES = 3


penalty = 0.5
epsilon = 1e-06


def dequantize(values, indices, lookup):
    levels = lookup.shape[0]
    onehot = (indices[:, :, None] == jnp.arange(levels, dtype=jnp.int32)).astype(jnp.float32)
    scales = jnp.dot(onehot, lookup, precision=lax.Precision.HIGHEST)
    groups = indices.shape[0]
    widened = (
        values.reshape(groups, values.shape[0] // groups, values.shape[1]).astype(jnp.float32)
        * scales[:, None, :]
    )
    return widened.reshape(values.shape).astype(jnp.bfloat16)


def slot_layout(variant_ids, var_width, var_count):
    holder = variant_ids // var_width
    column = variant_ids % var_width
    owner_marks = (holder[..., None] == jnp.arange(var_count, dtype=jnp.int32)).astype(jnp.int32)
    before = jnp.cumsum(owner_marks, axis=-2) - owner_marks
    serial = jnp.sum(before * owner_marks, -1)
    return (holder, column, serial)


def block_update(gradient, coeffs, inverse):
    phenos, fit_width = gradient.shape
    blocks, block_size = (inverse.shape[0], inverse.shape[1])
    inner_term = (gradient - penalty * coeffs).reshape(phenos, blocks, block_size)
    direction = jnp.einsum("bij,pbj->pbi", inverse, inner_term, precision=lax.Precision.HIGHEST)
    return direction.reshape(phenos, fit_width).astype(jnp.bfloat16)


def on_device(
    geno, scale_index, scale_table, residual, beta_active, block_inverse, active_ids, admit_ids
):
    var_count = lax.axis_size("var")
    var_rank = lax.axis_index("var")
    samp_rows, var_width = geno.shape
    inv_root = 1.0 / math.sqrt(samp_rows * lax.axis_size("samp"))
    phenos = residual.shape[0]
    local_ids = jnp.concatenate([active_ids, admit_ids])
    fit_width = local_ids.shape[0]
    capacity = 2 * fit_width // var_count
    dequant = dequantize(geno, scale_index, scale_table)
    resid_low = residual.astype(jnp.bfloat16)
    screened = (
        lax.psum(jnp.dot(resid_low, dequant, preferred_element_type=jnp.float32), "samp") * inv_root
    )
    all_ids = lax.all_gather(local_ids, "var", axis=0, tiled=True).reshape(var_count, fit_width)
    holder, column, serial = slot_layout(all_ids, var_width, var_count)
    held_here = holder == var_rank
    wanted = held_here[:, None, :] & (
        serial[:, None, :] == jnp.arange(capacity, dtype=jnp.int32)[None, :, None]
    )
    source_column = jnp.sum(jnp.where(wanted, column[:, None, :], 0), -1).reshape(-1)
    present = jnp.any(wanted, -1).reshape(-1)
    selected = jnp.where(
        present[None, :], jnp.take(dequant, source_column, axis=1), jnp.zeros((), jnp.bfloat16)
    )
    position = lax.dynamic_index_in_dim(holder * capacity + serial, var_rank, 0, keepdims=False)
    coeffs = jnp.concatenate([beta_active, jnp.zeros((phenos, admit_ids.shape[0]), jnp.float32)], 1)
    current = residual
    for pass_index in range(PASSES):
        partial_sums = lax.psum(
            jnp.dot(resid_low, selected, preferred_element_type=jnp.float32), "samp"
        )
        routed = lax.all_to_all(partial_sums, "var", split_axis=1, concat_axis=1, tiled=True)
        gradient = jnp.take(routed, position, axis=1) * inv_root
        direction = block_update(gradient, coeffs, block_inverse)
        placed = (
            jnp.zeros((phenos, var_count * capacity), jnp.bfloat16).at[:, position].set(direction)
        )
        returned = lax.all_to_all(placed, "var", split_axis=1, concat_axis=1, tiled=True)
        partial_update = jnp.einsum(
            "pc,sc->ps", returned, selected, preferred_element_type=jnp.float32
        )
        update = lax.psum(partial_update, "var") * inv_root
        cross_sum, square = lax.psum(
            (jnp.sum(current * update, 1), jnp.sum(update * update, 1)), "samp"
        )
        factor = (cross_sum / (square + epsilon))[:, None]
        current = current - factor * update
        coeffs = coeffs + factor * direction.astype(jnp.float32)
        if pass_index + 1 < PASSES:
            resid_low = current.astype(jnp.bfloat16)
    return (screened, coeffs, current)


def solution(mesh):
    placed = (
        P("samp", "var"),
        P("samp", "var"),
        P(),
        P(None, "samp"),
        P(None, "var"),
        P("var", None, None),
        P("var"),
        P("var"),
    )
    return jax.shard_map(
        on_device,
        mesh=mesh,
        in_specs=placed,
        out_specs=(P(None, "var"), P(None, "var"), P(None, "samp")),
        check_vma=False,
    )
```

profile of v0, /device:TPU:0, one launch (start us, length us, event | category | flops | bytes accessed | tf_op | source)
XLA Modules:
  0.0 450.3 jit_solution(15364064158792349478)
XLA Ops:
  10.1 12.3 %copy.78 = bf16[2048,2048]{0,1:T(8,128)(2,1)} copy(bf16[2048,2048]{1,0:T(8,128)(2,1)} %param.10) | data formatting | bytes 16777216 | tf_op args[0]
  22.5 14.5 %all-gather = s32[8,1,512]{2,1,0:T(1,128)S(1)} all-gather(s32[1,1,512]{2,1,0:T(1,128)S(1)} %bitcast.157), channel_id=1, replica_groups=mesh['var'=8,'samp'=4] {'var'}, dimensions={0}, use_global_device_ids=true | all-gather | bytes 18432 | tf_op jit(solution)/shard_map/all_gather | solution.py:60
  37.0 9.0 %reduce-window.6 = s32[8,8,4,128]{3,1,2,0:T(8,128)S(1)} reduce-window(s32[8,8,4,128]{3,1,2,0:T(8,128)S(1)} %fusion.13, s32[]{:T(128)} %constant.73.clone.1), window={size=1x1x1x128 pad=0_0x0_0x0_0x127_0}, to_apply=%region_1.2 | reduce-window | flops 4161536 | bytes 262148 | tf_op jit(solution)/shard_map/reduce-window
  47.6 4.6 %mul.124 = f32[16,128,2048]{1,0,2:T(8,128)S(1)} broadcast(f32[16,2048]{0,1:T(8,128)S(1)} %bitcast.133), dimensions={0,2} | broadcast | bytes 16908288 | tf_op jit(solution)/shard_map/mul | solution.py:21
  52.2 9.2 %fusion = bf16[2048,2048]{0,1:T(8,128)(2,1)} fusion(f32[256,8,16,128]{3,2,1,0:T(8,128)S(1)} %bitcast.130, bf16[2048,2048]{0,1:T(8,128)(2,1)S(1)} %bitcast.132), kind=kLoop, calls=%fused_computation.8 | loop fusion | flops 12582912 | bytes 33554432 | tf_op jit(solution)/shard_map/convert_element_type | solution.py:24
  61.4 13.3 %gather_fusion = bf16[1024,2048]{1,0:T(8,128)(2,1)} fusion(bf16[2048,2048]{0,1:T(8,128)(2,1)} %fusion, s32[1024]{0:T(1024)S(1)} %broadcast_clamp_fusion), kind=kCustom, calls=%fused_computation.3 | custom fusion | bytes 8392704 | tf_op jit(solution)/shard_map/jit(_take)/gather | solution.py:69
  80.6 16.9 %psum.92 = f32[8,8,128]{2,0,1:T(8,128)} all-reduce(f32[8,8,128]{2,0,1:T(8,128)S(1)} %convolution_bitcast_fusion.3), channel_id=1, replica_groups=mesh['var'=8,'samp'=4] {'samp'}, use_global_device_ids=true, to_apply=%region_6.7 | all-reduce | flops 8192 | bytes 65536 | tf_op jit(solution)/shard_map/psum | solution.py:75
  101.2 5.5 %all-to-all-done = f32[8,8,128]{2,0,1:T(8,128)S(1)} async-done(((f32[8,8,128]{2,0,1:T(8,128)}), f32[8,8,128]{2,0,1:T(8,128)S(1)}, u32[]{:S(2)}, u32[]{:S(2)}) %all-to-all-start) | async-done | bytes 32800 | tf_op jit(solution)/shard_map/all_to_all | solution.py:78
  110.7 8.0 %all_to_all.72 = bf16[8,8,128]{2,0,1:T(8,128)(2,1)S(1)} all-to-all(bf16[8,8,128]{2,0,1:T(8,128)(2,1)S(1)} %copy.84), channel_id=1, replica_groups=mesh['var'=8,'samp'=4] {'var'}, dimensions={1} | all-to-all | bytes 32768 | tf_op jit(solution)/shard_map/all_to_all | solution.py:84
  118.7 3.5 fusion.24
  122.2 51.3 %all-reduce.11.cloned.1.call-done = f32[8,2048]{1,0:T(8,128)} async-done(((f32[8,2048]{1,0:T(8,128)}), f32[8,2048]{1,0:T(8,128)}) %all-reduce.11.cloned.1.call-update) | async-done | bytes 65552 | tf_op jit(solution)/shard_map/psum | solution.py:88
  174.5 9.8 %all-reduce.3 = (f32[8]{0:T(128)S(1)}, f32[8]{0:T(128)S(1)}) all-reduce(f32[8]{0:T(128)S(1)} %get-tuple-element.21, f32[8]{0:T(128)S(1)} %get-tuple-element.20), channel_id=1, replica_groups=mesh['var'=8,'samp'=4] {'samp'}, use_global_device_ids=true, to_apply=%region_10.12 | all-reduce | flops 16 | bytes 128 | tf_op jit(solution)/shard_map/psum | solution.py:89
  188.7 14.4 %psum.96 = f32[8,8,128]{2,0,1:T(8,128)S(1)} all-reduce(f32[8,8,128]{2,0,1:T(8,128)S(1)} %convolution_bitcast_fusion.2), channel_id=1, replica_groups=mesh['var'=8,'samp'=4] {'samp'}, use_global_device_ids=true, to_apply=%region_13.15 | all-reduce | flops 8192 | bytes 65536 | tf_op jit(solution)/shard_map/psum | solution.py:75
  203.0 8.3 %all_to_all.73 = f32[8,8,128]{2,0,1:T(8,128)S(1)} all-to-all(f32[8,8,128]{2,0,1:T(8,128)S(1)} %psum.96), channel_id=1, replica_groups=mesh['var'=8,'samp'=4] {'var'}, dimensions={1} | all-to-all | bytes 65536 | tf_op jit(solution)/shard_map/all_to_all | solution.py:78
  215.4 8.0 %all_to_all.74 = bf16[8,8,128]{2,0,1:T(8,128)(2,1)S(1)} all-to-all(bf16[8,8,128]{2,0,1:T(8,128)(2,1)S(1)} %copy.88), channel_id=1, replica_groups=mesh['var'=8,'samp'=4] {'var'}, dimensions={1} | all-to-all | bytes 32768 | tf_op jit(solution)/shard_map/all_to_all | solution.py:84
  223.4 3.5 fusion.21
  226.9 52.2 %all-reduce.13.cloned.1.call-done = f32[8,2048]{1,0:T(8,128)} async-done(((f32[8,2048]{1,0:T(8,128)}), f32[8,2048]{1,0:T(8,128)}) %all-reduce.13.cloned.1.call-update) | async-done | bytes 65552 | tf_op jit(solution)/shard_map/psum | solution.py:88
  280.1 9.8 %all-reduce.2 = (f32[8]{0:T(128)S(1)}, f32[8]{0:T(128)S(1)}) all-reduce(f32[8]{0:T(128)S(1)} %get-tuple-element.19, f32[8]{0:T(128)S(1)} %get-tuple-element.18), channel_id=1, replica_groups=mesh['var'=8,'samp'=4] {'samp'}, use_global_device_ids=true, to_apply=%region_17.19 | all-reduce | flops 16 | bytes 128 | tf_op jit(solution)/shard_map/psum | solution.py:89
  294.3 14.4 %psum.100 = f32[8,8,128]{2,0,1:T(8,128)S(1)} all-reduce(f32[8,8,128]{2,0,1:T(8,128)S(1)} %convolution_bitcast_fusion.1), channel_id=1, replica_groups=mesh['var'=8,'samp'=4] {'samp'}, use_global_device_ids=true, to_apply=%region_20.22 | all-reduce | flops 8192 | bytes 65536 | tf_op jit(solution)/shard_map/psum | solution.py:75
  308.6 8.3 %all_to_all.75 = f32[8,8,128]{2,0,1:T(8,128)S(1)} all-to-all(f32[8,8,128]{2,0,1:T(8,128)S(1)} %psum.100), channel_id=1, replica_groups=mesh['var'=8,'samp'=4] {'var'}, dimensions={1} | all-to-all | bytes 65536 | tf_op jit(solution)/shard_map/all_to_all | solution.py:78
  325.2 6.3 %convolution_bitcast_fusion = f32[8,2048]{1,0:T(8,128)} fusion(bf16[2048,2048]{0,1:T(8,128)(2,1)} %fusion, f32[8,2048]{1,0:T(8,128)S(1)} %copy-done.2), kind=kOutput, calls=%fused_computation.10 | convolution fusion | flops 67125248 | bytes 8519680 | tf_op jit(solution)/shard_map/dot_general | solution.py:58
  335.1 38.0 %all-reduce.9.cloned.1.call-done = f32[8,2048]{1,0:T(8,128)} async-done(((f32[8,2048]{1,0:T(8,128)}), f32[8,2048]{1,0:T(8,128)}) %all-reduce.9.cloned.1.call-update) | async-done | bytes 65552 | tf_op jit(solution)/shard_map/psum | solution.py:58
  374.6 55.2 %all-reduce.15.cloned.1.call-done = f32[8,2048]{1,0:T(8,128)} async-done(((f32[8,2048]{1,0:T(8,128)}), f32[8,2048]{1,0:T(8,128)}) %all-reduce.15.cloned.1.call-update) | async-done | bytes 65552 | tf_op jit(solution)/shard_map/psum | solution.py:88
  430.8 9.8 %all-reduce.1 = (f32[8]{0:T(128)S(1)}, f32[8]{0:T(128)S(1)}) all-reduce(f32[8]{0:T(128)S(1)} %get-tuple-element.17, f32[8]{0:T(128)S(1)} %get-tuple-element.16), channel_id=1, replica_groups=mesh['var'=8,'samp'=4] {'samp'}, use_global_device_ids=true, to_apply=%region_24.26 | all-reduce | flops 16 | bytes 128 | tf_op jit(solution)/shard_map/psum | solution.py:89
  (90 shorter events, 48.4 us)
Async XLA Ops:
  8.0 100.0 %copy-start = (f32[2,256,256]{2,1,0:T(8,128)S(1)}, f32[2,256,256]{2,1,0:T(8,128)}, u32[]{:S(2)}) copy-start(f32[2,256,256]{2,1,0:T(8,128)} %param.15) | copy-start | bytes 1572868
  10.0 12.4 %copy-start.4 = (s32[448]{0:T(512)S(1)}, s32[448]{0:T(512)}, u32[]{:S(2)}) copy-start(s32[448]{0:T(512)} %param.16) | copy-start | bytes 5380
  10.0 12.3 %copy-start.5 = (s32[64]{0:T(128)S(1)}, s32[64]{0:T(128)}, u32[]{:S(2)}) copy-start(s32[64]{0:T(128)} %param.17) | copy-start | bytes 772
  46.5 5.7 %slice-start = ((s8[8388608]{0:T(1024)(128)(4,1)}), s8[4194304]{0:T(1024)(128)(4,1)S(1)}, s32[]{:S(2)}) async-start(s8[8388608]{0:T(1024)(128)(4,1)} %bitcast.131), calls=%async_computation.10 | async-start | bytes 8388608
  47.6 4.6 %slice-start.1 = ((s8[8388608]{0:T(1024)(128)(4,1)}), s8[4194304]{0:T(1024)(128)(4,1)S(1)}, s32[]{:S(2)}) async-start(s8[8388608]{0:T(1024)(128)(4,1)} %bitcast.131), calls=%async_computation.11 | async-start | bytes 8388608
  74.7 4.8 %copy-start.2 = (f32[8,2048]{1,0:T(8,128)S(1)}, f32[8,2048]{1,0:T(8,128)}, u32[]{:S(2)}) copy-start(f32[8,2048]{1,0:T(8,128)} %param.13) | copy-start | bytes 196612
  77.5 2.0 copy-start.1
  79.5 28.5 %copy-start.3 = (f32[8,448]{1,0:T(8,128)S(1)}, f32[8,448]{1,0:T(8,128)}, u32[]{:S(2)}) copy-start(f32[8,448]{1,0:T(8,128)} %param.14) | copy-start | bytes 43012
  97.5 9.1 %all-to-all-start = ((f32[8,8,128]{2,0,1:T(8,128)}), f32[8,8,128]{2,0,1:T(8,128)S(1)}, u32[]{:S(2)}, u32[]{:S(2)}) async-start(f32[8,8,128]{2,0,1:T(8,128)} %psum.92), calls=%async_computation | async-start | bytes 65536 | tf_op jit(solution)/shard_map/all_to_all | solution.py:78
  100.9 72.6 %all-reduce.11.cloned.1.call-start = ((), (), s32[]{:S(2)}) async-start(), calls=%async_computation.7 | async-start | bytes 131072 | tf_op jit(solution)/shard_map/psum | solution.py:88
  122.2 156.9 %all-reduce.13.cloned.1.call-start = ((), (), s32[]{:S(2)}) async-start(), calls=%async_computation.8 | async-start | bytes 131072 | tf_op jit(solution)/shard_map/psum | solution.py:88
  321.6 10.0 %all-to-all-start.5 = ((bf16[8,8,128]{2,0,1:T(8,128)(2,1)}), bf16[8,8,128]{2,0,1:T(8,128)(2,1)S(1)}, u32[]{:S(2)}, u32[]{:S(2)}) async-start(bf16[8,8,128]{2,0,1:T(8,128)(2,1)} %copy.92), calls=%async_computation.5 | async-start | bytes 32768 | tf_op jit(solution)/shard_map/all_to_all | solution.py:84
  325.0 48.1 %all-reduce.9.cloned.1.call-start = ((), (), s32[]{:S(2)}) async-start(), calls=%async_computation.6 | async-start | bytes 131072 | tf_op jit(solution)/shard_map/psum | solution.py:58
  331.5 98.2 %all-reduce.15.cloned.1.call-start = ((), (), s32[]{:S(2)}) async-start(), calls=%async_computation.9 | async-start | bytes 131072 | tf_op jit(solution)/shard_map/psum | solution.py:88
Sparse Core Ops, SparseCore 0:
  122.3 51.1 all-reduce.10
  227.0 52.0 all-reduce.12
Sparse Core Ops, SparseCore 1:
  331.6 41.4 all-reduce.8
  375.3 54.4 all-reduce.14
where the time goes:
time: 452 us; the launch traced here: 450 us
  waiting for transfers between devices  202 us (45%)
  blocking collectives  122 us (27%)
  local copies, waits for them, and re-layouts  43.8 us (10%)
  other arithmetic  31 us (7%)
  matrix products  27.8 us (6%)
  between operations  15.9 us (4%)
  starting transfers between devices  7.27 us (2%)
    psum x3, waiting for transfers between devices, on_device(): update = lax.psum(partial_update, 'var') * inv_root  159 us
    psum x3, blocking collectives, on_device(): lax.psum(jnp.dot(resid_low, selected, preferred_element_type=jnp.float32)...  45.6 us
    psum x1, waiting for transfers between devices, on_device(): lax.psum(jnp.dot(resid_low, dequant, preferred_element_type=jnp.float32),...  38 us
    psum x3, blocking collectives, on_device(): lax.psum((jnp.sum(current * update, 1), jnp.sum(update * update, 1)), 'sa...  29.5 us
    all_to_all x2, blocking collectives, on_device(): lax.all_to_all(partial_sums, 'var', split_axis=1, concat_axis=1, tiled=True)  16.6 us
    all_to_all x2, blocking collectives, on_device(): lax.all_to_all(placed, 'var', split_axis=1, concat_axis=1, tiled=True)  16 us
    all_gather x1, blocking collectives, on_device(): lax.all_gather(local_ids, 'var', axis=0, tiled=True)  14.5 us
    unnamed x17, local copies, waits for them, and re-layouts  14.3 us
  transfers between devices with their start and end apart: 6, of which 5 were waited for; matrix products, arithmetic and copies ran while one was open for 2% of the time, Pallas kernels for 0%

commit v1 on v0

v1 whole, which is shorter than its diff:
```python
import functools
import math

import jax
import jax.numpy as jnp
from jax import lax
from jax.experimental import pallas as pl
from jax.experimental.pallas import tpu as pltpu
from jax.sharding import PartitionSpec as P

PASSES = 3
PENALTY = 0.5
EPSILON = 1e-06
LANES = 128
F32 = jnp.float32
BF16 = jnp.bfloat16
NN = (((1,), (0,)), ((), ()))
NT = (((1,), (1,)), ((), ()))


def dot(a, b, dims=NN):
    return lax.dot_general(a, b, dims, preferred_element_type=F32)


def split(x):
    high = x.astype(BF16).astype(F32)
    return jnp.concatenate([high, x - high], axis=0).astype(BF16)


def joined(x):
    half = x.shape[0] // 2
    return x[:half] + x[half:]


def kernel(
    V, S, pad,
    geno, sidx, table, resid, beta, binv, ids_in,
    scores_out, coef_out, resid_out,
    x_ref, scale_ref, rlow, part, pick, unpick, tri, inv_hi, inv_lo, ids_all, src_row,
    packed, d_got, d_held, up_two, coef, grad, direct, own_up,
    send_a, recv_a, send_b, recv_b, send_c, recv_c, recv_u, recv_p, send_s, recv_s,
    load_sem, send_sem, recv_sem,
):
    N = V * S
    rows, width = x_ref.shape
    groups = sidx.shape[0]
    per_group = rows // groups
    levels = table.shape[0]
    ph = resid.shape[0]
    fit = ids_in.shape[1]
    blocks, bsize = binv.shape[0], binv.shape[1]
    chunk = rows // V
    step = 2 * per_group
    n_steps = rows // step
    inv_root = 1.0 / math.sqrt(rows * S)
    mv, ms = lax.axis_index("var"), lax.axis_index("samp")
    me = ms * V + mv

    def load(i):
        at = pl.ds(pl.multiple_of(i * step, step), step)
        return pltpu.make_async_copy(geno.at[at], x_ref.at[at], load_sem.at[i])

    for i in range(n_steps):
        load(i).start()

    barrier = pltpu.get_barrier_semaphore()

    def other(k):
        t = lax.rem(me + k, N)
        return lax.div(t, V), lax.rem(t, V)

    def greet(k, c):
        s, v = other(k)
        pl.semaphore_signal(
            barrier, inc=1, device_id={"var": v, "samp": s}, device_id_type=pl.DeviceIdType.MESH
        )
        return c

    lax.fori_loop(1, N, greet, 0)

    def send(src, dst, sem, v, s):
        pltpu.make_async_remote_copy(
            src_ref=src, dst_ref=dst, send_sem=send_sem.at[sem], recv_sem=recv_sem.at[sem],
            device_id={"var": v, "samp": s}, device_id_type=pl.DeviceIdType.MESH,
        ).start()

    def got(ref, sem):
        pltpu.make_async_copy(ref, ref, recv_sem.at[sem]).wait()

    def sent(ref, sem):
        pltpu.make_async_copy(ref, ref, send_sem.at[sem]).wait()

    def var_peers(fn):
        def one(k, c):
            fn(lax.rem(mv + k, V))
            return c

        lax.fori_loop(1, V, one, 0)

    IDS, A, B, C, U, SC, SM = 0, 1, 1 + PASSES, 1 + 2 * PASSES, 1 + 3 * PASSES, 1 + 4 * PASSES, 2 + 4 * PASSES

    ids_all[mv] = ids_in[...]
    index = sidx[...]
    scales = jnp.zeros(index.shape, F32)
    for level in range(levels):
        scales = jnp.where(index == level, table[level], scales)
    scale_ref[...] = scales
    rlow[...] = resid[...].astype(BF16)
    for b in range(blocks):
        whole = binv[b]
        high = whole.astype(BF16)
        inv_hi[b] = high
        inv_lo[b] = (whole - high.astype(F32)).astype(BF16)
    kept = beta.shape[1]
    coef[...] = jnp.zeros((ph, fit), F32)
    coef[:, 0:kept] = beta[...]
    tri[...] = jnp.where(
        lax.broadcasted_iota(jnp.int32, (fit, fit), 0) < lax.broadcasted_iota(jnp.int32, (fit, fit), 1),
        1.0, 0.0,
    ).astype(BF16)

    pl.semaphore_wait(barrier, N - 1)
    var_peers(lambda v: send(ids_all.at[mv], ids_all.at[mv], IDS, v, ms))

    part[...] = jnp.zeros((ph, width), F32)
    cols = 512

    def screen(i, c):
        load(i).wait()
        for half in range(2):
            at = pl.ds(pl.multiple_of(i * step + half * per_group, per_group), per_group)
            for j in range(width // cols):
                lane = slice(j * cols, (j + 1) * cols)
                scale = scale_ref[pl.ds(2 * i + half, 1), lane]
                x_ref[at, lane] = (x_ref[at, lane].astype(F32) * scale).astype(BF16)
        at = pl.ds(pl.multiple_of(i * step, step), step)
        part[...] += dot(rlow[:, at], x_ref[at, :])
        return c

    lax.fori_loop(0, n_steps, screen, 0)
    recv_p[ms] = part[...]

    got(ids_all.at[pl.ds(0, V - 1)], IDS)
    line = lax.broadcasted_iota(jnp.int32, (V, fit), 0)
    all_ids = jnp.zeros((V, fit), jnp.int32)
    for g in range(V):
        all_ids = jnp.where(line == g, ids_all[g][0:1], all_ids)
    column = all_ids - mv * width
    held = (column >= 0) & (column < width)
    serial = dot(jnp.where(held, 1.0, 0.0).astype(BF16), tri[...]).astype(jnp.int32)
    serial = jnp.where(held, serial, -1)
    column = jnp.where(held, column, 0)
    eight = lax.broadcasted_iota(jnp.int32, (8, fit), 0)
    turn = lax.broadcasted_iota(jnp.int32, (pad, fit), 0)
    for g in range(V):
        col = column[g:g + 1]
        digits = jnp.where(
            eight == 0, lax.shift_right_logical(col, 7),
            jnp.where(eight == 1, col & 127, jnp.where(eight == 2, 1, 0)),
        ).astype(F32).astype(BF16)
        place = jnp.where(turn == serial[g:g + 1], 1.0, 0.0).astype(BF16)
        found = dot(digits, place, NT)
        where = jnp.where(found[2:3] > 0.5, found[0:1] * 128.0 + found[1:2], -1.0)
        src_row[g] = jnp.broadcast_to(where.astype(jnp.int32), (8, pad))

    def mark(i, c):
        at = pl.ds(pl.multiple_of(i * 256, 256), 256)
        here = lax.broadcasted_iota(jnp.int32, (256, pad), 0) + i * 256
        for g in range(V):
            pick[at, g * pad:(g + 1) * pad] = jnp.where(here == src_row[g][0:1], 1.0, 0.0).astype(BF16)
        return c

    lax.fori_loop(0, width // 256, mark, 0)

    mine = ids_in[0:1] - line * width
    marks = jnp.where((mine >= 0) & (mine < width), 1.0, 0.0)
    before = dot(marks.astype(BF16), tri[...])
    position = jnp.sum(marks * (before + line.astype(F32) * float(pad)), axis=0, keepdims=True)
    position = position.astype(jnp.int32)

    def place_own(i, c):
        at = pl.ds(pl.multiple_of(i * 128, 128), 128)
        here = lax.broadcasted_iota(jnp.int32, (128, fit), 0) + i * 128
        unpick[at, :] = jnp.where(here == position, 1.0, 0.0).astype(BF16)
        return c

    lax.fori_loop(0, V * pad // 128, place_own, 0)

    resid_out[...] = resid[...]
    lane = lax.broadcasted_iota(jnp.int32, (ph, LANES), 1)

    def length(total):
        return total[:, 0:1] / (total[:, 1:2] + EPSILON)

    def step_sums(p):
        cur = resid_out[:, pl.ds(pl.multiple_of(mv * chunk, chunk), chunk)]
        upd = own_up[...]
        cross = jnp.sum(cur * upd, axis=1, keepdims=True)
        square = jnp.sum(upd * upd, axis=1, keepdims=True)
        return jnp.where(lane == 0, cross, jnp.where(lane == 1, square, 0.0))

    def advance(factor, p):
        for v in range(V):
            at = slice(v * chunk, (v + 1) * chunk)
            resid_out[:, at] = resid_out[:, at] - factor * recv_u[p, v]

    sums = jnp.zeros((ph, LANES), F32)
    for p in range(PASSES):
        up_two[...] = split(part[...])
        wide = 2 * pad

        for n in range(V * pad // wide):
            out = joined(dot(up_two[...], pick[:, n * wide:(n + 1) * wide]))
            for q in range(2):
                send_a[p, 2 * n + q, 0:ph] = out[:, q * pad:(q + 1) * pad]
                send_a[p, 2 * n + q, ph:2 * ph] = jnp.broadcast_to(sums, (ph, LANES))

        def route(k, c):
            s, v = other(k)
            send(send_a.at[p, v], recv_a.at[p, me], A + p, v, s)
            return c

        lax.fori_loop(1, N, route, 0)
        recv_a[p, me] = send_a[p, mv]
        if p == 0:
            def share(k, c):
                send(recv_p.at[ms], recv_p.at[ms], SC, mv, lax.rem(ms + k, S))
                return c

            lax.fori_loop(1, S, share, 0)
        got(recv_a.at[p, pl.ds(0, N - 1)], A + p)
        for v in range(V):
            val = recv_a[p, v, 0:ph]
            for s in range(1, S):
                val = val + recv_a[p, s * V + v, 0:ph]
            packed[:, v * pad:(v + 1) * pad] = split(val)
        slots = joined(dot(packed[...], unpick[...])) * inv_root
        if p == 0:
            grad[...] = slots
        else:
            total = recv_a[p, 0, ph:2 * ph]
            for n in range(1, N):
                total = total + recv_a[p, n, ph:2 * ph]
            factor = length(total)
            grad[...] = grad[...] - factor * slots
            coef[...] = coef[...] + factor * direct[...].astype(F32)
        inner = grad[...] - PENALTY * coef[...]
        for b in range(blocks):
            at = slice(b * bsize, (b + 1) * bsize)
            two = split(inner[:, at])
            main = joined(dot(two, inv_hi[b], NT))
            rest = dot(two, inv_lo[b], NT)
            direct[:, at] = (main + rest[:ph]).astype(BF16)

        back = dot(direct[...], unpick[...], NT)
        for v in range(V):
            send_b[p, v] = back[:, v * pad:(v + 1) * pad]
        var_peers(lambda v: send(send_b.at[p, v], recv_b.at[p, mv], B + p, v, ms))
        recv_b[p, mv] = send_b[p, mv]
        if p > 0:
            advance(factor, p - 1)
        got(recv_b.at[p, pl.ds(0, V - 1)], B + p)
        for v in range(V):
            d_got[:, v * pad:(v + 1) * pad] = recv_b[p, v].astype(BF16)
        def spread(i, c):
            at = pl.ds(pl.multiple_of(i * 512, 512), 512)
            d_held[:, at] = dot(d_got[...], pick[at, :], NT).astype(BF16)
            return c

        lax.fori_loop(0, width // 512, spread, 0)

        def piece(v):
            at = pl.ds(pl.multiple_of(v * chunk, chunk), chunk)
            return dot(d_held[...], x_ref[at, :], NT)

        def give(v):
            send_c[p, v] = piece(v)
            send(send_c.at[p, v], recv_c.at[p, mv], C + p, v, ms)

        var_peers(give)
        recv_c[p, mv] = piece(mv)
        got(recv_c.at[p, pl.ds(0, V - 1)], C + p)
        val = recv_c[p, 0]
        for v in range(1, V):
            val = val + recv_c[p, v]
        val = val * inv_root
        own_up[...] = val
        recv_u[p, mv] = val
        sums = step_sums(p)
        if p + 1 == PASSES:
            send_s[...] = sums
            recv_s[me] = sums

            def tell(k, c):
                s, v = other(k)
                send(send_s, recv_s.at[me], SM, v, s)
                return c

            var_peers(lambda v: send(recv_u.at[p, mv], recv_u.at[p, mv], U + p, v, ms))
            lax.fori_loop(1, N, tell, 0)
        else:
            var_peers(lambda v: send(recv_u.at[p, mv], recv_u.at[p, mv], U + p, v, ms))
        got(recv_u.at[p, pl.ds(0, V - 1)], U + p)
        if p + 1 < PASSES:
            for v in range(V):
                up_two[:, v * chunk:(v + 1) * chunk] = split(recv_u[p, v])

            def project(i, c):
                at = pl.ds(pl.multiple_of(i * 256, 256), 256)
                part[:, at] = joined(dot(up_two[...], x_ref[:, at]))
                return c

            lax.fori_loop(0, width // 256, project, 0)

    got(recv_p.at[pl.ds(0, S - 1)], SC)
    val = recv_p[0]
    for s in range(1, S):
        val = val + recv_p[s]
    scores_out[...] = val * inv_root
    got(recv_s.at[pl.ds(0, N - 1)], SM)
    total = recv_s[0]
    for n in range(1, N):
        total = total + recv_s[n]
    factor = length(total)
    advance(factor, PASSES - 1)
    coef_out[...] = coef[...] + factor * direct[...].astype(F32)

    sent(ids_all.at[pl.ds(0, V - 1)], IDS)
    sent(recv_p.at[pl.ds(0, S - 1)], SC)
    sent(recv_s.at[pl.ds(0, N - 1)], SM)
    for p in range(PASSES):
        sent(recv_a.at[p, pl.ds(0, N - 1)], A + p)
        sent(recv_b.at[p, pl.ds(0, V - 1)], B + p)
        sent(recv_c.at[p, pl.ds(0, V - 1)], C + p)
        sent(recv_u.at[p, pl.ds(0, V - 1)], U + p)


def on_device(geno, scale_index, scale_table, residual, beta_active, block_inverse, active_ids, admit_ids):
    V, S = lax.axis_size("var"), lax.axis_size("samp")
    N = V * S
    rows, width = geno.shape
    ph = residual.shape[0]
    ids = jnp.concatenate([active_ids, admit_ids])
    fit = ids.shape[0]
    pad = LANES * pl.cdiv(2 * fit // V, LANES)
    ids = jnp.broadcast_to(ids[None, :], (8, fit))
    chunk = rows // V
    vmem = pl.BlockSpec(memory_space=pltpu.VMEM)
    n_sem = 3 + 4 * PASSES
    return pl.pallas_call(
        functools.partial(kernel, V, S, pad),
        out_shape=(
            jax.ShapeDtypeStruct((ph, width), F32),
            jax.ShapeDtypeStruct((ph, fit), F32),
            jax.ShapeDtypeStruct((ph, rows), F32),
        ),
        in_specs=[
            pl.BlockSpec(memory_space=pl.ANY), vmem, pl.BlockSpec(memory_space=pltpu.SMEM),
            vmem, vmem, vmem, vmem,
        ],
        out_specs=(vmem, vmem, vmem),
        scratch_shapes=[
            pltpu.VMEM((rows, width), BF16),
            pltpu.VMEM(scale_index.shape, F32),
            pltpu.VMEM((ph, rows), BF16),
            pltpu.VMEM((ph, width), F32),
            pltpu.VMEM((width, V * pad), BF16),
            pltpu.VMEM((V * pad, fit), BF16),
            pltpu.VMEM((fit, fit), BF16),
            pltpu.VMEM(block_inverse.shape, BF16),
            pltpu.VMEM(block_inverse.shape, BF16),
            pltpu.VMEM((V, 8, fit), jnp.int32),
            pltpu.VMEM((V, 8, pad), jnp.int32),
            pltpu.VMEM((2 * ph, V * pad), BF16),
            pltpu.VMEM((ph, V * pad), BF16),
            pltpu.VMEM((ph, width), BF16),
            pltpu.VMEM((2 * ph, width), BF16),
            pltpu.VMEM((ph, fit), F32),
            pltpu.VMEM((ph, fit), F32),
            pltpu.VMEM((ph, fit), BF16),
            pltpu.VMEM((ph, chunk), F32),
            pltpu.VMEM((PASSES, V, 2 * ph, pad), F32),
            pltpu.VMEM((PASSES, N, 2 * ph, pad), F32),
            pltpu.VMEM((PASSES, V, ph, pad), F32),
            pltpu.VMEM((PASSES, V, ph, pad), F32),
            pltpu.VMEM((PASSES, V, ph, chunk), F32),
            pltpu.VMEM((PASSES, V, ph, chunk), F32),
            pltpu.VMEM((PASSES, V, ph, chunk), F32),
            pltpu.VMEM((S, ph, width), F32),
            pltpu.VMEM((ph, LANES), F32),
            pltpu.VMEM((N, ph, LANES), F32),
            pltpu.SemaphoreType.DMA((rows // (2 * (rows // scale_index.shape[0])),)),
            pltpu.SemaphoreType.DMA((n_sem,)),
            pltpu.SemaphoreType.DMA((n_sem,)),
        ],
        compiler_params=pltpu.CompilerParams(
            collective_id=0, has_side_effects=True, vmem_limit_bytes=60 * 1024 * 1024
        ),
    )(geno, scale_index, scale_table, residual, beta_active, block_inverse, ids)


def solution(mesh):
    placed = (
        P("samp", "var"), P("samp", "var"), P(), P(None, "samp"), P(None, "var"),
        P("var", None, None), P("var"), P("var"),
    )
    return jax.shard_map(
        on_device, mesh=mesh, in_specs=placed,
        out_specs=(P(None, "var"), P(None, "var"), P(None, "samp")), check_vma=False,
    )
```

time: 452 us -> 102 us (0.23)
  waiting for transfers between devices: 202 us -> 0 us
  blocking collectives: 122 us -> 0 us
  Pallas kernels: 0 us -> 95.4 us
  local copies, waits for them, and re-layouts: 43.8 us -> 4.88 us
  other arithmetic: 31 us -> 0.77 us
  matrix products: 27.8 us -> 0 us
  between operations: 15.9 us -> 0.64 us
  starting transfers between devices: 7.27 us -> 0 us
    psum x4 -> x0, waiting for transfers between devices: 197 us -> none  [the longest x3 159 us: on_device(): update = lax.psum(partial_update, 'var') * inv_root]
    pallas_call x0 -> x1, Pallas kernels: none -> 95.4 us  [on_device(): pl.pallas_call(functools.partial(kernel, V, S, pad), out_shape=(jax.Shape...]
    psum x6 -> x0, blocking collectives: 75.2 us -> none  [the longest x3 45.6 us: on_device(): lax.psum(jnp.dot(resid_low, selected, preferred_element_type=jnp.float32)...]
    all_to_all x4 -> x0, blocking collectives: 32.6 us -> none  [the longest x2 16.6 us: on_device(): lax.all_to_all(partial_sums, 'var', split_axis=1, concat_axis=1, tiled=True)]
    dot_general x11 -> x0, matrix products: 27.8 us -> none  [the longest x3 10.4 us: on_device(): jnp.einsum('pc,sc->ps', returned, selected, preferred_element_type=jnp.fl...]
    gather x7 -> x0, local copies, waits for them, and re-layouts: 16.7 us -> none  [the longest x1 13.3 us: on_device(): jnp.take(dequant, source_column, axis=1)]
    all_gather x1 -> x0, blocking collectives: 14.5 us -> none  [on_device(): lax.all_gather(local_ids, 'var', axis=0, tiled=True)]
    unnamed x17 -> x3, local copies, waits for them, and re-layouts: 14.3 us -> 4.27 us
  transfers between devices with their start and end apart: 6 -> 0, of which waited for: 5 -> 0; matrix products, arithmetic and copies ran while one was open for 2% -> 0% of each run, Pallas kernels for 0% -> 0%
where the time goes in v1:
time: 102 us
  Pallas kernels  95.4 us (94%)
  local copies, waits for them, and re-layouts  4.88 us (5%)
    pallas_call x1, Pallas kernels, on_device(): pl.pallas_call(functools.partial(kernel, V, S, pad), out_shape=(jax.Shape...  95.4 us
    unnamed x3, local copies, waits for them, and re-layouts  4.27 us

profile of v1, /device:TPU:0, one launch (start us, length us, event | category | flops | bytes accessed | tf_op | source)
XLA Modules:
  0.0 101.7 jit_solution(3561980158056805152)
XLA Ops:
  0.6 0.8 pad_add_fusion
  1.4 0.6 broadcast_in_dim.2.ids_in
  2.0 95.4 %shard_map.103 = (f32[8,2048]{1,0:T(8,128)}, f32[8,512]{1,0:T(8,128)}, f32[8,2048]{1,0:T(8,128)}) custom-call(bf16[2048,2048]{1,0:T(8,128)(2,1)} %geno.1, s32[16,2048]{1,0:T(8,128)} %sidx.1, f32[16]{0:T(128)} %table.1, f32[8,2048]{1,0:T(8,128)} %resid.1, f32[8,448]{1,0:T(8,128)} %beta.1, f32[2,256,256]{2,1,0:T(8,128)} %binv.1, s32[8,512]{1,0:T(8,128)} %broadcast_in_dim.2.ids_in), custom_call_target="tpu_custom_call" | custom-call | tf_op jit(solution)/shard_map/pallas_call | solution.py:350
  97.5 1.5 %copy.14 = f32[8,2048]{1,0:T(8,128)} copy(f32[8,2048]{1,0:T(8,128)} %get-tuple-element.6) | data formatting | bytes 131072
  98.9 1.3 %copy.15 = f32[8,512]{1,0:T(8,128)} copy(f32[8,512]{1,0:T(8,128)} %get-tuple-element.7) | data formatting | bytes 32768
  100.3 1.5 %copy.16 = f32[8,2048]{1,0:T(8,128)} copy(f32[8,2048]{1,0:T(8,128)} %get-tuple-element.8) | data formatting | bytes 131072

commit v2 on v1

--- a/solution.py
+++ b/solution.py
@@ -34,11 +34,11 @@
 
 def kernel(
     V, S, pad,
-    geno, sidx, table, resid, beta, binv, ids_in,
+    geno, sidx, table, resid, beta, binv, active, admit,
     scores_out, coef_out, resid_out,
     x_ref, scale_ref, rlow, part, pick, unpick, tri, inv_hi, inv_lo, ids_all, src_row,
-    packed, d_got, d_held, up_two, coef, grad, direct, own_up,
-    send_a, recv_a, send_b, recv_b, send_c, recv_c, recv_u, recv_p, send_s, recv_s,
+    packed, d_got, d_held, up_two, coef, grad, direct,
+    send_a, recv_a, send_b, recv_b, send_c, recv_c, recv_u, recv_p, recv_s,
     load_sem, send_sem, recv_sem,
 ):
     N = V * S
@@ -47,7 +47,8 @@
     per_group = rows // groups
     levels = table.shape[0]
     ph = resid.shape[0]
-    fit = ids_in.shape[1]
+    kept = active.shape[1]
+    fit = kept + admit.shape[1]
     blocks, bsize = binv.shape[0], binv.shape[1]
     chunk = rows // V
     step = 2 * per_group
@@ -99,7 +100,8 @@
 
     IDS, A, B, C, U, SC, SM = 0, 1, 1 + PASSES, 1 + 2 * PASSES, 1 + 3 * PASSES, 1 + 4 * PASSES, 2 + 4 * PASSES
 
-    ids_all[mv] = ids_in[...]
+    ids_all[mv, :, 0:kept] = jnp.broadcast_to(active[...], (8, kept))
+    ids_all[mv, :, kept:fit] = jnp.broadcast_to(admit[...], (8, fit - kept))
     index = sidx[...]
     scales = jnp.zeros(index.shape, F32)
     for level in range(levels):
@@ -111,7 +113,6 @@
         high = whole.astype(BF16)
         inv_hi[b] = high
         inv_lo[b] = (whole - high.astype(F32)).astype(BF16)
-    kept = beta.shape[1]
     coef[...] = jnp.zeros((ph, fit), F32)
     coef[:, 0:kept] = beta[...]
     tri[...] = jnp.where(
@@ -172,7 +173,7 @@
 
     lax.fori_loop(0, width // 256, mark, 0)
 
-    mine = ids_in[0:1] - line * width
+    mine = ids_all[mv][0:1] - line * width
     marks = jnp.where((mine >= 0) & (mine < width), 1.0, 0.0)
     before = dot(marks.astype(BF16), tri[...])
     position = jnp.sum(marks * (before + line.astype(F32) * float(pad)), axis=0, keepdims=True)
@@ -189,22 +190,35 @@
     resid_out[...] = resid[...]
     lane = lax.broadcasted_iota(jnp.int32, (ph, LANES), 1)
 
-    def length(total):
+    def length(p):
+        got(recv_s.at[p, pl.ds(0, S - 1)], SM + p)
+        total = recv_s[p, 0]
+        for s in range(1, S):
+            total = total + recv_s[p, s]
         return total[:, 0:1] / (total[:, 1:2] + EPSILON)
 
-    def step_sums(p):
-        cur = resid_out[:, pl.ds(pl.multiple_of(mv * chunk, chunk), chunk)]
-        upd = own_up[...]
-        cross = jnp.sum(cur * upd, axis=1, keepdims=True)
-        square = jnp.sum(upd * upd, axis=1, keepdims=True)
-        return jnp.where(lane == 0, cross, jnp.where(lane == 1, square, 0.0))
+    def tell_sums(p):
+        cross = jnp.zeros((ph, chunk), F32)
+        square = jnp.zeros((ph, chunk), F32)
+        for v in range(V):
+            upd = recv_u[p, v]
+            cross = cross + resid_out[:, v * chunk:(v + 1) * chunk] * upd
+            square = square + upd * upd
+        cross = jnp.sum(cross, axis=1, keepdims=True)
+        square = jnp.sum(square, axis=1, keepdims=True)
+        recv_s[p, ms] = jnp.where(lane == 0, cross, jnp.where(lane == 1, square, 0.0))
+
+        def tell(k, c):
+            send(recv_s.at[p, ms], recv_s.at[p, ms], SM + p, mv, lax.rem(ms + k, S))
+            return c
+
+        lax.fori_loop(1, S, tell, 0)
 
     def advance(factor, p):
         for v in range(V):
             at = slice(v * chunk, (v + 1) * chunk)
             resid_out[:, at] = resid_out[:, at] - factor * recv_u[p, v]
 
-    sums = jnp.zeros((ph, LANES), F32)
     for p in range(PASSES):
         up_two[...] = split(part[...])
         wide = 2 * pad
@@ -212,8 +226,7 @@
         for n in range(V * pad // wide):
             out = joined(dot(up_two[...], pick[:, n * wide:(n + 1) * wide]))
             for q in range(2):
-                send_a[p, 2 * n + q, 0:ph] = out[:, q * pad:(q + 1) * pad]
-                send_a[p, 2 * n + q, ph:2 * ph] = jnp.broadcast_to(sums, (ph, LANES))
+                send_a[p, 2 * n + q] = out[:, q * pad:(q + 1) * pad].astype(BF16)
 
         def route(k, c):
             s, v = other(k)
@@ -230,18 +243,15 @@
             lax.fori_loop(1, S, share, 0)
         got(recv_a.at[p, pl.ds(0, N - 1)], A + p)
         for v in range(V):
-            val = recv_a[p, v, 0:ph]
+            val = recv_a[p, v].astype(F32)
             for s in range(1, S):
-                val = val + recv_a[p, s * V + v, 0:ph]
+                val = val + recv_a[p, s * V + v].astype(F32)
             packed[:, v * pad:(v + 1) * pad] = split(val)
         slots = joined(dot(packed[...], unpick[...])) * inv_root
         if p == 0:
             grad[...] = slots
         else:
-            total = recv_a[p, 0, ph:2 * ph]
-            for n in range(1, N):
-                total = total + recv_a[p, n, ph:2 * ph]
-            factor = length(total)
+            factor = length(p - 1)
             grad[...] = grad[...] - factor * slots
             coef[...] = coef[...] + factor * direct[...].astype(F32)
         inner = grad[...] - PENALTY * coef[...]
@@ -254,14 +264,14 @@
 
         back = dot(direct[...], unpick[...], NT)
         for v in range(V):
-            send_b[p, v] = back[:, v * pad:(v + 1) * pad]
+            send_b[p, v] = back[:, v * pad:(v + 1) * pad].astype(BF16)
         var_peers(lambda v: send(send_b.at[p, v], recv_b.at[p, mv], B + p, v, ms))
         recv_b[p, mv] = send_b[p, mv]
         if p > 0:
             advance(factor, p - 1)
         got(recv_b.at[p, pl.ds(0, V - 1)], B + p)
         for v in range(V):
-            d_got[:, v * pad:(v + 1) * pad] = recv_b[p, v].astype(BF16)
+            d_got[:, v * pad:(v + 1) * pad] = recv_b[p, v]
         def spread(i, c):
             at = pl.ds(pl.multiple_of(i * 512, 512), 512)
             d_held[:, at] = dot(d_got[...], pick[at, :], NT).astype(BF16)
@@ -274,33 +284,20 @@
             return dot(d_held[...], x_ref[at, :], NT)
 
         def give(v):
-            send_c[p, v] = piece(v)
+            send_c[p, v] = piece(v).astype(BF16)
             send(send_c.at[p, v], recv_c.at[p, mv], C + p, v, ms)
 
         var_peers(give)
-        recv_c[p, mv] = piece(mv)
+        recv_c[p, mv] = piece(mv).astype(BF16)
         got(recv_c.at[p, pl.ds(0, V - 1)], C + p)
-        val = recv_c[p, 0]
+        val = recv_c[p, 0].astype(F32)
         for v in range(1, V):
-            val = val + recv_c[p, v]
+            val = val + recv_c[p, v].astype(F32)
         val = val * inv_root
-        own_up[...] = val
         recv_u[p, mv] = val
-        sums = step_sums(p)
-        if p + 1 == PASSES:
-            send_s[...] = sums
-            recv_s[me] = sums
-
-            def tell(k, c):
-                s, v = other(k)
-                send(send_s, recv_s.at[me], SM, v, s)
-                return c
-
-            var_peers(lambda v: send(recv_u.at[p, mv], recv_u.at[p, mv], U + p, v, ms))
-            lax.fori_loop(1, N, tell, 0)
-        else:
-            var_peers(lambda v: send(recv_u.at[p, mv], recv_u.at[p, mv], U + p, v, ms))
+        var_peers(lambda v: send(recv_u.at[p, mv], recv_u.at[p, mv], U + p, v, ms))
         got(recv_u.at[p, pl.ds(0, V - 1)], U + p)
+        tell_sums(p)
         if p + 1 < PASSES:
             for v in range(V):
                 up_two[:, v * chunk:(v + 1) * chunk] = split(recv_u[p, v])
@@ -317,19 +314,15 @@
     for s in range(1, S):
         val = val + recv_p[s]
     scores_out[...] = val * inv_root
-    got(recv_s.at[pl.ds(0, N - 1)], SM)
-    total = recv_s[0]
-    for n in range(1, N):
-        total = total + recv_s[n]
-    factor = length(total)
+    factor = length(PASSES - 1)
     advance(factor, PASSES - 1)
     coef_out[...] = coef[...] + factor * direct[...].astype(F32)
 
     sent(ids_all.at[pl.ds(0, V - 1)], IDS)
     sent(recv_p.at[pl.ds(0, S - 1)], SC)
-    sent(recv_s.at[pl.ds(0, N - 1)], SM)
     for p in range(PASSES):
         sent(recv_a.at[p, pl.ds(0, N - 1)], A + p)
+        sent(recv_s.at[p, pl.ds(0, S - 1)], SM + p)
         sent(recv_b.at[p, pl.ds(0, V - 1)], B + p)
         sent(recv_c.at[p, pl.ds(0, V - 1)], C + p)
         sent(recv_u.at[p, pl.ds(0, V - 1)], U + p)
@@ -340,13 +333,11 @@
     N = V * S
     rows, width = geno.shape
     ph = residual.shape[0]
-    ids = jnp.concatenate([active_ids, admit_ids])
-    fit = ids.shape[0]
+    fit = active_ids.shape[0] + admit_ids.shape[0]
     pad = LANES * pl.cdiv(2 * fit // V, LANES)
-    ids = jnp.broadcast_to(ids[None, :], (8, fit))
     chunk = rows // V
     vmem = pl.BlockSpec(memory_space=pltpu.VMEM)
-    n_sem = 3 + 4 * PASSES
+    n_sem = 2 + 5 * PASSES
     return pl.pallas_call(
         functools.partial(kernel, V, S, pad),
         out_shape=(
@@ -356,7 +347,7 @@
         ),
         in_specs=[
             pl.BlockSpec(memory_space=pl.ANY), vmem, pl.BlockSpec(memory_space=pltpu.SMEM),
-            vmem, vmem, vmem, vmem,
+            vmem, vmem, vmem, vmem, vmem,
         ],
         out_specs=(vmem, vmem, vmem),
         scratch_shapes=[
@@ -378,17 +369,15 @@
             pltpu.VMEM((ph, fit), F32),
             pltpu.VMEM((ph, fit), F32),
             pltpu.VMEM((ph, fit), BF16),
-            pltpu.VMEM((ph, chunk), F32),
-            pltpu.VMEM((PASSES, V, 2 * ph, pad), F32),
-            pltpu.VMEM((PASSES, N, 2 * ph, pad), F32),
-            pltpu.VMEM((PASSES, V, ph, pad), F32),
-            pltpu.VMEM((PASSES, V, ph, pad), F32),
-            pltpu.VMEM((PASSES, V, ph, chunk), F32),
-            pltpu.VMEM((PASSES, V, ph, chunk), F32),
+            pltpu.VMEM((PASSES, V, ph, pad), BF16),
+            pltpu.VMEM((PASSES, N, ph, pad), BF16),
+            pltpu.VMEM((PASSES, V, ph, pad), BF16),
+            pltpu.VMEM((PASSES, V, ph, pad), BF16),
+            pltpu.VMEM((PASSES, V, ph, chunk), BF16),
+            pltpu.VMEM((PASSES, V, ph, chunk), BF16),
             pltpu.VMEM((PASSES, V, ph, chunk), F32),
             pltpu.VMEM((S, ph, width), F32),
-            pltpu.VMEM((ph, LANES), F32),
-            pltpu.VMEM((N, ph, LANES), F32),
+            pltpu.VMEM((PASSES, S, ph, LANES), F32),
             pltpu.SemaphoreType.DMA((rows // (2 * (rows // scale_index.shape[0])),)),
             pltpu.SemaphoreType.DMA((n_sem,)),
             pltpu.SemaphoreType.DMA((n_sem,)),
@@ -396,7 +385,7 @@
         compiler_params=pltpu.CompilerParams(
             collective_id=0, has_side_effects=True, vmem_limit_bytes=60 * 1024 * 1024
         ),
-    )(geno, scale_index, scale_table, residual, beta_active, block_inverse, ids)
+    )(geno, scale_index, scale_table, residual, beta_active, block_inverse, active_ids[None], admit_ids[None])
 
 
 def solution(mesh):

time: 102 us -> 90 us (0.88)
  Pallas kernels: 95.4 us -> 84.8 us
    pallas_call x1, Pallas kernels: 95.4 us -> 84.8 us  [on_device(): pl.pallas_call(functools.partial(kernel, V, S, pad), out_shape=(jax.Shape...]
where the time goes in v2:
time: 90 us; the launch traced here: 89.7 us
  Pallas kernels  84.8 us (94%)
  local copies, waits for them, and re-layouts  4.27 us (5%)
    pallas_call x1, Pallas kernels, on_device(): pl.pallas_call(functools.partial(kernel, V, S, pad), out_shape=(jax.Shape...  84.8 us
    unnamed x3, local copies, waits for them, and re-layouts  4.27 us

profile of v2, /device:TPU:0, one launch (start us, length us, event | category | flops | bytes accessed | tf_op | source)
XLA Modules:
  0.0 89.7 jit_solution(2442704529966290641)
XLA Ops:
  0.6 84.8 %shard_map.103 = (f32[8,2048]{1,0:T(8,128)}, f32[8,512]{1,0:T(8,128)}, f32[8,2048]{1,0:T(8,128)}) custom-call(bf16[2048,2048]{1,0:T(8,128)(2,1)} %geno.1, s32[16,2048]{1,0:T(8,128)} %sidx.1, f32[16]{0:T(128)} %table.1, f32[8,2048]{1,0:T(8,128)} %resid.1, f32[8,448]{1,0:T(8,128)} %beta.1, f32[2,256,256]{2,1,0:T(8,128)} %binv.1, s32[1,448]{1,0:T(1,128)} %bitcast.2, ...), custom_call_target="tpu_custom_call" | custom-call | tf_op jit(solution)/shard_map/pallas_call | solution.py:341
  85.5 1.5 %copy.14 = f32[8,2048]{1,0:T(8,128)} copy(f32[8,2048]{1,0:T(8,128)} %get-tuple-element.6) | data formatting | bytes 131072
  87.0 1.3 %copy.15 = f32[8,512]{1,0:T(8,128)} copy(f32[8,512]{1,0:T(8,128)} %get-tuple-element.7) | data formatting | bytes 32768
  88.3 1.5 %copy.16 = f32[8,2048]{1,0:T(8,128)} copy(f32[8,2048]{1,0:T(8,128)} %get-tuple-element.8) | data formatting | bytes 131072
